TPU v7x, 32 devices: a whole 2x2x4 slice. The times are simulated.
32 devices in a mesh: member: 2 (over x), dp: 16 (over z, y, core).
Axes of the slice: x: 2, y: 2, z: 4, core: 2. Of those that a mesh axis runs over, the one named last changes fastest.
Arguments:
- residual: bfloat16 [512, 3072], P(('member', 'dp')), parts along dimension 0, may hold values from -6 to 6
- upstream: bfloat16 [512, 3072], P(('member', 'dp')), parts along dimension 0, may hold values from -6 to 6
- gate_weight: bfloat16 [6144, 10240], P('member', 'dp'), parts along dimension 0, may hold values from -0.109375 to 0.109375
- up_weight: bfloat16 [6144, 10240], P('member', 'dp'), parts along dimension 0, may hold values from -0.109375 to 0.109375
- down_weight: bfloat16 [20480, 3072], P(('member', 'dp')), parts along dimension 0, may hold values from -0.0625 to 0.0625
- gain: float32 [6144], P('member'), parts along dimension 0, may hold values from 0.25 to 1.75
Outputs:
- grad_residual: bfloat16 [512, 3072], P(('member', 'dp')), parts along dimension 0
- grad_gate: bfloat16 [6144, 10240], P('member', 'dp'), parts along dimension 0
- grad_up: bfloat16 [6144, 10240], P('member', 'dp'), parts along dimension 0
- grad_down: bfloat16 [20480, 3072], P(('member', 'dp')), parts along dimension 0
- grad_gain: float32 [6144], P('member'), parts along dimension 0
There are 2 independent parts, one for each index of `member`. A program takes and returns all parts, laid end to end along the dimension named above; each array names one. Nothing has to cross between parts.
All inputs are finite; a program needn't handle non-finite values.
Results may differ from a plain program's by a relative error of at most 0.0068.
Values may be sent and summed in bfloat16 or wider, within the bound.
No kernel may reach another device: no remote copies, remote signals or barrier semaphores. Data moves between devices by JAX's collectives and lax.ppermute only.
A program may use at most 128 MiB of HBM per device.

v0:
```python
import jax
import jax.numpy as jnp
from jax import lax
from jax.sharding import PartitionSpec as P

norm_floor = 0.5
gelu_coeff = 0.7978845608
cubic_term = 0.044715


def gelu_parts(gate_out):
    inner = jnp.tanh(gelu_coeff * (gate_out + cubic_term * gate_out * gate_out * gate_out))
    activated = 0.5 * gate_out * (1.0 + inner)
    gelu_slope = 0.5 * (1.0 + inner) + 0.5 * gate_out * (1.0 - inner * inner) * gelu_coeff * (
        1.0 + 3.0 * cubic_term * gate_out * gate_out
    )
    return (activated, gelu_slope)


def contract_last(left, right):
    return lax.dot_general(
        left, right, (((1,), (1,)), ((), ())), preferred_element_type=jnp.float32
    )


def contract_first(left, right):
    return lax.dot_general(
        left, right, (((0,), (0,)), ((), ())), preferred_element_type=jnp.float32
    )


def per_device(residual, upstream, gate_weight, up_weight, down_weight, gain):
    widened = residual.astype(jnp.float32)
    norm_scale = lax.rsqrt(jnp.mean(widened * widened, axis=1, keepdims=True) + norm_floor)
    unit_rows = widened * norm_scale
    normed = (unit_rows * gain).astype(jnp.bfloat16)
    normed_all = lax.all_gather(normed, "dp", axis=0, tiled=True)
    gate_out = jnp.dot(normed_all, gate_weight, preferred_element_type=jnp.float32)
    up_out = jnp.dot(normed_all, up_weight, preferred_element_type=jnp.float32)
    activated, gelu_slope = gelu_parts(gate_out)
    hidden = (activated * up_out).astype(jnp.bfloat16)
    upstream_all = lax.all_gather(upstream, "dp", axis=0, tiled=True)
    hidden_grad = contract_last(upstream_all, down_weight)
    grad_down = contract_first(hidden, upstream_all).astype(jnp.bfloat16)
    gate_grad = (hidden_grad * up_out * gelu_slope).astype(jnp.bfloat16)
    up_grad = (hidden_grad * activated).astype(jnp.bfloat16)
    grad_gate = contract_first(normed_all, gate_grad).astype(jnp.bfloat16)
    grad_up = contract_first(normed_all, up_grad).astype(jnp.bfloat16)
    partial_grad = contract_last(gate_grad, gate_weight) + contract_last(up_grad, up_weight)
    normed_grad = lax.psum_scatter(partial_grad, "dp", scatter_dimension=0, tiled=True)
    unit_grad = normed_grad * gain
    inner_mean = jnp.mean(unit_grad * unit_rows, axis=1, keepdims=True)
    grad_residual = (
        upstream.astype(jnp.float32) + norm_scale * (unit_grad - unit_rows * inner_mean)
    ).astype(jnp.bfloat16)
    grad_gain = lax.psum(jnp.sum(normed_grad * unit_rows, axis=0), "dp")
    return (grad_residual, grad_gate, grad_up, grad_down, grad_gain)


def solution(mesh):
    placed = (
        P(("member", "dp"), None),
        P(("member", "dp"), None),
        P("member", "dp"),
        P("member", "dp"),
        P(("member", "dp"), None),
        P("member"),
    )
    return jax.shard_map(
        per_device,
        mesh=mesh,
        in_specs=placed,
        out_specs=(
            P(("member", "dp"), None),
            P("member", "dp"),
            P("member", "dp"),
            P(("member", "dp"), None),
            P("member"),
        ),
        check_vma=False,
    )
```

profile of v0, /device:TPU:0, one launch (start us, length us, event | category | flops | bytes accessed | tf_op | source)
XLA Modules:
  0.0 235.7 jit_solution(8409215572186535631)
XLA Ops:
  7.2 0.0 all-gather.5.cloned.1.call-start
  7.2 1.0 fusion.18
  8.3 1.6 fusion.11
  9.9 0.0 all-gather.5.cloned.1.call-update
  9.9 0.0 all-gather.3.cloned.1.call-start
  10.0 0.7 all-gather.3.cloned.1.call-update
  10.7 0.0 reduce-scatter.2.cloned.1.call-start
  10.7 42.5 %all-gather.5.cloned.1.call-done = bf16[256,3072]{1,0:T(8,128)(2,1)} async-done(((bf16[16,3072]{1,0:T(8,128)(2,1)}), bf16[256,3072]{1,0:T(8,128)(2,1)}) %all-gather.5.cloned.1.call-update) | async-done | bytes 1572880 | tf_op jit(solution)/shard_map/all_gather | solution.py:37
  53.2 0.0 copy-start
  53.2 4.1 %fusion.24 = f32[256,640]{1,0:T(8,128)S(1)} fusion(bf16[256,3072]{1,0:T(8,128)(2,1)} %all-gather.5.cloned.1.call-done, bf16[3072,640]{1,0:T(8,128)(2,1)} %param.8), kind=kOutput, calls=%fused_computation.37 | convolution fusion | flops 1006632960 | bytes 6160384 | tf_op jit(solution)/shard_map/dot_general | solution.py:38
  57.3 0.0 copy-done
  57.3 0.1 copy-done.2
  57.4 1.5 fusion.23
  58.9 34.9 %all-gather.3.cloned.1.call-done = bf16[256,3072]{1,0:T(8,128)(2,1)} async-done(((bf16[16,3072]{1,0:T(8,128)(2,1)}), bf16[256,3072]{1,0:T(8,128)(2,1)}) %all-gather.3.cloned.1.call-update) | async-done | bytes 1572880 | tf_op jit(solution)/shard_map/all_gather | solution.py:42
  93.8 4.4 %multiply_convert_fusion.1 = (bf16[256,640]{1,0:T(8,128)(2,1)S(1)}, bf16[256,640]{1,0:T(8,128)(2,1)S(1)}) fusion(f32[256,640]{1,0:T(8,128)S(1)} %fusion.24, f32[256,640]{1,0:T(8,128)S(1)} %fusion.23, bf16[256,3072]{1,0:T(8,128)(2,1)} %all-gather.3.cloned.1.call-done, bf16[640,3072]{1,0:T(8,128)(2,1)} %param.10), kind=kOutput, calls=%fused_computation.14 | convolution fusion | flops 1010401280 | bytes 7471104 | tf_op jit(solution)/shard_map/dot_general | solution.py:21
  98.3 0.0 copy-start.3
  98.3 0.0 copy-done.1
  98.3 1.4 fusion.25
  99.7 0.7 copy-done.3
  100.4 3.1 %convolution_add_fusion = f32[256,3072]{1,0:T(8,128)} fusion(f32[256,3072]{1,0:T(8,128)S(1)} %fusion.25, bf16[256,640]{1,0:T(8,128)(2,1)S(1)} %get-tuple-element.7, bf16[3072,640]{1,0:T(8,128)(2,1)S(1)} %copy-done.3), kind=kOutput, calls=%fused_computation.3 | convolution fusion | flops 1007419392 | bytes 10551296 | tf_op jit(solution)/shard_map/dot_general | solution.py:21
  103.4 0.0 reduce-scatter.2.cloned.1.call-update
  103.5 3.4 %convolution_convert_fusion.1 = bf16[3072,640]{1,0:T(8,128)(2,1)} fusion(bf16[256,3072]{1,0:T(8,128)(2,1)S(1)} %copy-done, bf16[256,640]{1,0:T(8,128)(2,1)S(1)} %get-tuple-element.7), kind=kOutput, calls=%fused_computation.1 | convolution fusion | flops 1008599040 | bytes 5832704 | tf_op jit(solution)/shard_map/dot_general | solution.py:27
  106.8 3.4 %convolution_convert_fusion.2 = bf16[3072,640]{1,0:T(8,128)(2,1)} fusion(bf16[256,3072]{1,0:T(8,128)(2,1)S(1)} %copy-done, bf16[256,640]{1,0:T(8,128)(2,1)S(1)} %get-tuple-element.8), kind=kOutput, calls=%fused_computation.2 | convolution fusion | flops 1008599040 | bytes 5832704 | tf_op jit(solution)/shard_map/dot_general | solution.py:27
  110.2 0.0 copy-done.5
  110.2 3.3 %convolution_convert_fusion = bf16[640,3072]{1,0:T(8,128)(2,1)} fusion(bf16[256,3072]{1,0:T(8,128)(2,1)S(1)} %copy-done.5, f32[256,640]{1,0:T(8,128)S(1)} %fusion.23, f32[256,640]{1,0:T(8,128)S(1)} %fusion.24), kind=kOutput, calls=%fused_computation | convolution fusion | flops 1010237440 | bytes 6815744 | tf_op jit(solution)/shard_map/dot_general | solution.py:27
  113.5 55.1 %reduce-scatter.2.cloned.1.call-done = f32[16,3072]{1,0:T(8,128)} async-done(((f32[256,3072]{1,0:T(8,128)}), f32[16,3072]{1,0:T(8,128)}) %reduce-scatter.2.cloned.1.call-update) | async-done | bytes 196624 | tf_op jit(solution)/shard_map/reduce_scatter | solution.py:50
  168.6 0.0 copy-done.4
  168.6 0.0 copy-done.7
  168.6 1.2 fusion.17
  169.8 57.7 %psum.7 = f32[3072]{0:T(1024)} all-reduce(f32[3072]{0:T(1024)S(1)} %get-tuple-element.5), channel_id=1, replica_groups=mesh['member'=2,'dp'=16] {'dp'}, use_global_device_ids=true, to_apply=%region_4.0 | all-reduce | flops 3072 | bytes 24576 | tf_op jit(solution)/shard_map/psum | solution.py:56
  227.5 0.0 copy-done.6
  227.5 1.7 fusion.16
  (8 shorter events, 0.0 us)
Async XLA Ops:
  7.2 46.0 %all-gather.5.cloned.1.call-start = ((), (), s32[]{:S(2)}) async-start(), calls=%async_computation.2 | async-start | bytes 1671168 | tf_op jit(solution)/shard_map/all_gather | solution.py:37
  9.9 83.9 %all-gather.3.cloned.1.call-start = ((), (), s32[]{:S(2)}) async-start(), calls=%async_computation.1 | async-start | bytes 1671168 | tf_op jit(solution)/shard_map/all_gather | solution.py:42
  10.7 158.0 %reduce-scatter.2.cloned.1.call-start = ((), (), s32[]{:S(2)}) async-start(), calls=%async_computation.3 | async-start | bytes 3342336 | tf_op jit(solution)/shard_map/reduce_scatter | solution.py:50
  53.2 4.1 %copy-start = (bf16[256,3072]{1,0:T(8,128)(2,1)S(1)}, bf16[256,3072]{1,0:T(8,128)(2,1)}, u32[]{:S(2)}) copy-start(bf16[256,3072]{1,0:T(8,128)(2,1)} %all-gather.5.cloned.1.call-done) | copy-start | bytes 4718596
  53.2 4.2 %copy-start.2 = (bf16[3072,640]{1,0:T(8,128)(2,1)S(1)}, bf16[3072,640]{1,0:T(8,128)(2,1)}, u32[]{:S(2)}) copy-start(bf16[3072,640]{1,0:T(8,128)(2,1)} %param.9) | copy-start | bytes 11796484
  93.8 4.5 %copy-start.1 = (bf16[3072,640]{1,0:T(8,128)(2,1)S(1)}, bf16[3072,640]{1,0:T(8,128)(2,1)}, u32[]{:S(2)}) copy-start(bf16[3072,640]{1,0:T(8,128)(2,1)} %param.8) | copy-start | bytes 11796484
  98.3 2.1 copy-start.3
  106.8 3.4 %copy-start.5 = (bf16[256,3072]{1,0:T(8,128)(2,1)S(1)}, bf16[256,3072]{1,0:T(8,128)(2,1)}, u32[]{:S(2)}) copy-start(bf16[256,3072]{1,0:T(8,128)(2,1)} %all-gather.3.cloned.1.call-done) | copy-start | bytes 4718596
  110.2 58.4 %copy-start.4 = (bf16[16,3072]{1,0:T(8,128)(2,1)S(1)}, bf16[16,3072]{1,0:T(8,128)(2,1)}, u32[]{:S(2)}) copy-start(bf16[16,3072]{1,0:T(8,128)(2,1)} %param.6) | copy-start | bytes 294916
  110.2 58.4 %copy-start.7 = (f32[3072]{0:T(1024)S(1)}, f32[3072]{0:T(1024)}, u32[]{:S(2)}) copy-start(f32[3072]{0:T(1024)} %param.11) | copy-start | bytes 36868
  110.2 117.3 %copy-start.6 = (bf16[16,3072]{1,0:T(8,128)(2,1)S(1)}, bf16[16,3072]{1,0:T(8,128)(2,1)}, u32[]{:S(2)}) copy-start(bf16[16,3072]{1,0:T(8,128)(2,1)} %param.7) | copy-start | bytes 294916
Sparse Core Ops, SparseCore 0:
  10.8 42.3 all-gather.4
  55.5 38.2 all-gather.2
  103.6 64.9 reduce-scatter.1
where the time goes:
time: 236 us
  waiting for transfers between devices  133 us (56%)
  blocking collectives  57.7 us (24%)
  matrix products  24.5 us (10%)
  between operations  13.8 us (6%)
  other arithmetic  5.52 us (2%)
    psum x1, blocking collectives, per_device(): grad_gain = lax.psum(jnp.sum(normed_grad * unit_rows, axis=0), 'dp')  57.7 us
    reduce_scatter x1, waiting for transfers between devices, per_device(): lax.psum_scatter(partial_grad, 'dp', scatter_dimension=0, tiled=True)  55.1 us
    all_gather x1, waiting for transfers between devices, per_device(): normed_all = lax.all_gather(normed, 'dp', axis=0, tiled=True)  42.5 us
    all_gather x1, waiting for transfers between devices, per_device(): upstream_all = lax.all_gather(upstream, 'dp', axis=0, tiled=True)  34.9 us
    dot_general x3, matrix products, contract_first(): lax.dot_general(left, right, (((0,), (0,)), ((), ())), preferred_element_...  10.1 us
    dot_general x3, matrix products, contract_last(): lax.dot_general(left, right, (((1,), (1,)), ((), ())), preferred_element_...  8.91 us
  transfers between devices with their start and end apart: 3, of which 3 were waited for; matrix products, arithmetic and copies ran while one was open for 7% of the time, Pallas kernels for 0%

commit v1 on v0

--- a/solution.py
+++ b/solution.py
@@ -53,7 +53,9 @@
     grad_residual = (
         upstream.astype(jnp.float32) + norm_scale * (unit_grad - unit_rows * inner_mean)
     ).astype(jnp.bfloat16)
-    grad_gain = lax.psum(jnp.sum(normed_grad * unit_rows, axis=0), "dp")
+    own = jnp.sum(normed_grad * unit_rows, axis=0)
+    parts = lax.all_gather(own, "dp", axis=0, tiled=False)
+    grad_gain = parts.sum(axis=0)
     return (grad_residual, grad_gate, grad_up, grad_down, grad_gain)
 
 

time: 236 us -> 199 us (0.84)
  blocking collectives: 57.7 us -> 19.9 us
    psum x1 -> x0, blocking collectives: 57.7 us -> none  [per_device(): grad_gain = lax.psum(jnp.sum(normed_grad * unit_rows, axis=0), 'dp')]
    all_gather x0 -> x1, blocking collectives: none -> 19.9 us  [per_device(): parts = lax.all_gather(own, 'dp', axis=0, tiled=False)]
  transfers between devices with their start and end apart: 3 -> 3, of which waited for: 3 -> 3; matrix products, arithmetic and copies ran while one was open for 7% -> 8% of each run, Pallas kernels for 0% -> 0%
where the time goes in v1:
time: 199 us
  waiting for transfers between devices  133 us (67%)
  matrix products  24.5 us (12%)
  blocking collectives  19.9 us (10%)
  between operations  13.8 us (7%)
  other arithmetic  6.16 us (3%)
    reduce_scatter x1, waiting for transfers between devices, per_device(): lax.psum_scatter(partial_grad, 'dp', scatter_dimension=0, tiled=True)  55.1 us
    all_gather x1, waiting for transfers between devices, per_device(): normed_all = lax.all_gather(normed, 'dp', axis=0, tiled=True)  42.5 us
    all_gather x1, waiting for transfers between devices, per_device(): upstream_all = lax.all_gather(upstream, 'dp', axis=0, tiled=True)  34.9 us
    all_gather x1, blocking collectives, per_device(): parts = lax.all_gather(own, 'dp', axis=0, tiled=False)  19.9 us
    dot_general x3, matrix products, contract_first(): lax.dot_general(left, right, (((0,), (0,)), ((), ())), preferred_element_...  10.1 us
    dot_general x3, matrix products, contract_last(): lax.dot_general(left, right, (((1,), (1,)), ((), ())), preferred_element_...  8.91 us
    dot_general x1, matrix products, per_device(): jnp.dot(normed_all, gate_weight, preferred_element_type=jnp.float32)  4.12 us
  transfers between devices with their start and end apart: 3, of which 3 were waited for; matrix products, arithmetic and copies ran while one was open for 8% of the time, Pallas kernels for 0%

profile of v1, /device:TPU:0, one launch (start us, length us, event | category | flops | bytes accessed | tf_op | source)
XLA Modules:
  0.0 198.6 jit_solution(14411506833017218460)
XLA Ops:
  7.2 0.0 all-gather.6.cloned.1.call-start
  7.2 1.0 fusion.18
  8.3 1.6 fusion.11
  9.9 0.0 all-gather.6.cloned.1.call-update
  9.9 0.0 all-gather.4.cloned.1.call-start
  10.0 0.7 all-gather.4.cloned.1.call-update
  10.7 0.0 reduce-scatter.2.cloned.1.call-start
  10.7 42.5 %all-gather.6.cloned.1.call-done = bf16[256,3072]{1,0:T(8,128)(2,1)} async-done(((bf16[16,3072]{1,0:T(8,128)(2,1)}), bf16[256,3072]{1,0:T(8,128)(2,1)}) %all-gather.6.cloned.1.call-update) | async-done | bytes 1572880 | tf_op jit(solution)/shard_map/all_gather | solution.py:37
  53.2 4.1 %fusion.24 = f32[256,640]{1,0:T(8,128)S(1)} fusion(bf16[256,3072]{1,0:T(8,128)(2,1)} %all-gather.6.cloned.1.call-done, bf16[3072,640]{1,0:T(8,128)(2,1)} %param.8), kind=kOutput, calls=%fused_computation.37 | convolution fusion | flops 1006632960 | bytes 6160384 | tf_op jit(solution)/shard_map/dot_general | solution.py:38
  57.3 0.0 copy-done
  57.3 0.1 copy-done.2
  57.4 1.5 fusion.23
  58.9 34.9 %all-gather.4.cloned.1.call-done = bf16[256,3072]{1,0:T(8,128)(2,1)} async-done(((bf16[16,3072]{1,0:T(8,128)(2,1)}), bf16[256,3072]{1,0:T(8,128)(2,1)}) %all-gather.4.cloned.1.call-update) | async-done | bytes 1572880 | tf_op jit(solution)/shard_map/all_gather | solution.py:42
  93.8 4.4 %multiply_convert_fusion.1 = (bf16[256,640]{1,0:T(8,128)(2,1)S(1)}, bf16[256,640]{1,0:T(8,128)(2,1)S(1)}) fusion(f32[256,640]{1,0:T(8,128)S(1)} %fusion.24, f32[256,640]{1,0:T(8,128)S(1)} %fusion.23, bf16[256,3072]{1,0:T(8,128)(2,1)} %all-gather.4.cloned.1.call-done, bf16[640,3072]{1,0:T(8,128)(2,1)} %param.10), kind=kOutput, calls=%fused_computation.14 | convolution fusion | flops 1010401280 | bytes 7471104 | tf_op jit(solution)/shard_map/dot_general | solution.py:21
  98.3 0.0 copy-start.3
  98.3 0.0 copy-done.1
  98.3 1.4 fusion.25
  99.7 0.7 copy-done.3
  100.4 3.1 %convolution_add_fusion = f32[256,3072]{1,0:T(8,128)} fusion(f32[256,3072]{1,0:T(8,128)S(1)} %fusion.25, bf16[256,640]{1,0:T(8,128)(2,1)S(1)} %get-tuple-element.7, bf16[3072,640]{1,0:T(8,128)(2,1)S(1)} %copy-done.3), kind=kOutput, calls=%fused_computation.3 | convolution fusion | flops 1007419392 | bytes 10551296 | tf_op jit(solution)/shard_map/dot_general | solution.py:21
  103.4 0.0 reduce-scatter.2.cloned.1.call-update
  103.5 3.4 %convolution_convert_fusion.1 = bf16[3072,640]{1,0:T(8,128)(2,1)} fusion(bf16[256,3072]{1,0:T(8,128)(2,1)S(1)} %copy-done, bf16[256,640]{1,0:T(8,128)(2,1)S(1)} %get-tuple-element.7), kind=kOutput, calls=%fused_computation.1 | convolution fusion | flops 1008599040 | bytes 5832704 | tf_op jit(solution)/shard_map/dot_general | solution.py:27
  106.8 3.4 %convolution_convert_fusion.2 = bf16[3072,640]{1,0:T(8,128)(2,1)} fusion(bf16[256,3072]{1,0:T(8,128)(2,1)S(1)} %copy-done, bf16[256,640]{1,0:T(8,128)(2,1)S(1)} %get-tuple-element.8), kind=kOutput, calls=%fused_computation.2 | convolution fusion | flops 1008599040 | bytes 5832704 | tf_op jit(solution)/shard_map/dot_general | solution.py:27
  110.2 0.0 copy-done.5
  110.2 3.3 %convolution_convert_fusion = bf16[640,3072]{1,0:T(8,128)(2,1)} fusion(bf16[256,3072]{1,0:T(8,128)(2,1)S(1)} %copy-done.5, f32[256,640]{1,0:T(8,128)S(1)} %fusion.23, f32[256,640]{1,0:T(8,128)S(1)} %fusion.24), kind=kOutput, calls=%fused_computation | convolution fusion | flops 1010237440 | bytes 6815744 | tf_op jit(solution)/shard_map/dot_general | solution.py:27
  113.5 55.1 %reduce-scatter.2.cloned.1.call-done = f32[16,3072]{1,0:T(8,128)} async-done(((f32[256,3072]{1,0:T(8,128)}), f32[16,3072]{1,0:T(8,128)}) %reduce-scatter.2.cloned.1.call-update) | async-done | bytes 196624 | tf_op jit(solution)/shard_map/reduce_scatter | solution.py:50
  168.6 0.0 copy-done.4
  168.6 0.0 copy-done.7
  168.6 1.2 fusion.17
  169.8 19.9 %all-gather = f32[49152]{0:T(1024)S(1)} all-gather(f32[3072]{0:T(1024)S(1)} %get-tuple-element.5), channel_id=2, replica_groups=mesh['member'=2,'dp'=16] {'dp'}, dimensions={0}, use_global_device_ids=true | all-gather | bytes 208896 | tf_op jit(solution)/shard_map/all_gather | solution.py:57
  189.7 0.6 reduce_sum.39
  190.3 0.0 copy-done.6
  190.3 1.7 fusion.16
  (10 shorter events, 0.1 us)
Async XLA Ops:
  7.2 46.0 %all-gather.6.cloned.1.call-start = ((), (), s32[]{:S(2)}) async-start(), calls=%async_computation.2 | async-start | bytes 1671168 | tf_op jit(solution)/shard_map/all_gather | solution.py:37
  9.9 83.9 %all-gather.4.cloned.1.call-start = ((), (), s32[]{:S(2)}) async-start(), calls=%async_computation.1 | async-start | bytes 1671168 | tf_op jit(solution)/shard_map/all_gather | solution.py:42
  10.7 158.0 %reduce-scatter.2.cloned.1.call-start = ((), (), s32[]{:S(2)}) async-start(), calls=%async_computation.3 | async-start | bytes 3342336 | tf_op jit(solution)/shard_map/reduce_scatter | solution.py:50
  53.2 4.1 %copy-start = (bf16[256,3072]{1,0:T(8,128)(2,1)S(1)}, bf16[256,3072]{1,0:T(8,128)(2,1)}, u32[]{:S(2)}) copy-start(bf16[256,3072]{1,0:T(8,128)(2,1)} %all-gather.6.cloned.1.call-done) | copy-start | bytes 4718596
  53.2 4.2 %copy-start.2 = (bf16[3072,640]{1,0:T(8,128)(2,1)S(1)}, bf16[3072,640]{1,0:T(8,128)(2,1)}, u32[]{:S(2)}) copy-start(bf16[3072,640]{1,0:T(8,128)(2,1)} %param.9) | copy-start | bytes 11796484
  93.8 4.5 %copy-start.1 = (bf16[3072,640]{1,0:T(8,128)(2,1)S(1)}, bf16[3072,640]{1,0:T(8,128)(2,1)}, u32[]{:S(2)}) copy-start(bf16[3072,640]{1,0:T(8,128)(2,1)} %param.8) | copy-start | bytes 11796484
  98.3 2.1 %copy-start.3 = (bf16[3072,640]{1,0:T(8,128)(2,1)S(1)}, bf16[3072,640]{1,0:T(8,128)(2,1)}, u32[]{:S(2)}) copy-start(bf16[3072,640]{1,0:T(8,128)(2,1)} %param.9) | copy-start | bytes 11796484
  106.8 3.4 %copy-start.5 = (bf16[256,3072]{1,0:T(8,128)(2,1)S(1)}, bf16[256,3072]{1,0:T(8,128)(2,1)}, u32[]{:S(2)}) copy-start(bf16[256,3072]{1,0:T(8,128)(2,1)} %all-gather.4.cloned.1.call-done) | copy-start | bytes 4718596
  110.2 58.4 %copy-start.4 = (bf16[16,3072]{1,0:T(8,128)(2,1)S(1)}, bf16[16,3072]{1,0:T(8,128)(2,1)}, u32[]{:S(2)}) copy-start(bf16[16,3072]{1,0:T(8,128)(2,1)} %param.6) | copy-start | bytes 294916
  110.2 58.4 %copy-start.7 = (f32[3072]{0:T(1024)S(1)}, f32[3072]{0:T(1024)}, u32[]{:S(2)}) copy-start(f32[3072]{0:T(1024)} %param.11) | copy-start | bytes 36868
  110.2 80.1 %copy-start.6 = (bf16[16,3072]{1,0:T(8,128)(2,1)S(1)}, bf16[16,3072]{1,0:T(8,128)(2,1)}, u32[]{:S(2)}) copy-start(bf16[16,3072]{1,0:T(8,128)(2,1)} %param.7) | copy-start | bytes 294916
Sparse Core Ops, SparseCore 0:
  10.8 42.3 all-gather.5
  55.5 38.2 all-gather.3
  103.6 64.9 reduce-scatter.1
